TPU v7x, 256 devices: a 4x2x16 block of a 4x16x16 slice. The times are simulated.
256 devices in a mesh: groups: 2 (over y), patch: 16 (over z), cfg: 2 (over core), head: 4 (over x).
Axes of the slice: x: 4, y: 2, z: 16, core: 2. Of those that a mesh axis runs over, the one named last changes fastest.
The devices are a block of a 4x16x16 slice.
Arguments:
- img_hidden: bfloat16 [2, 8192, 3072], P('cfg', ('groups', 'patch')), parts along dimension 1, may hold values from -40 to 40
- txt_hidden: bfloat16 [2, 512, 3072], P('cfg', ('groups', 'patch')), parts along dimension 1, may hold values from -6 to 6
- modulation: float32 [4, 3, 3072], P(('groups', 'cfg')), parts along dimension 0, may hold values from -4 to 4
- w_qkv: bfloat16 [3072, 3, 1536], P(None, None, 'head'), may hold values from -0.109375 to 0.109375
- q_gain: float32 [128], replicated, may hold values from 1.2 to 2.5
- k_gain: float32 [128], replicated, may hold values from 1.2 to 2.5
- w_out: bfloat16 [1536, 3072], P('head'), may hold values from -0.15625 to 0.15625
- b_out: float32 [3072], replicated, may hold values from -3 to 3
- stale_kv: bfloat16 [2, 2, 8704, 1536], P('cfg', None, ('groups', 'patch'), 'head'), parts along dimension 2, may hold values from -500 to 500
- final_mod: float32 [4, 2, 3072], P(('groups', 'cfg')), parts along dimension 0, may hold values from -3 to 3
- w_final: bfloat16 [3072, 64], replicated, may hold values from -0.109375 to 0.109375
- b_final: float32 [64], replicated, may hold values from -3 to 3
- latent: float32 [8192, 64], P(('groups', 'patch', 'cfg', 'head')), parts along dimension 0, may hold values from -6 to 6
- prev_denoised: float32 [8192, 64], P(('groups', 'patch', 'cfg', 'head')), parts along dimension 0, may hold values from -24 to 24
- guidance: float32 [2], P('groups'), parts along dimension 0, may hold values from 2 to 5
- step_index: int32 [1], replicated, may hold values from 14 to 21
- step_count: int32 [1], replicated, may hold values from 24 to 27
Outputs:
- fresh_kv: bfloat16 [2, 2, 8704, 1536], P('cfg', None, ('groups', 'patch'), 'head'), parts along dimension 2
- next_latent: float32 [8192, 64], P(('groups', 'patch', 'cfg', 'head')), parts along dimension 0
- denoised: float32 [8192, 64], P(('groups', 'patch', 'cfg', 'head')), parts along dimension 0
There are 2 independent parts, one for each index of `groups`. A program takes and returns all parts, laid end to end along the dimension named above; an argument that names none is the same for every part. Nothing has to cross between parts.
All inputs are finite; a program needn't handle non-finite values.
Results may differ from a plain program's by a relative error of at most 0.0075.
The roundings to bfloat16 on the way count: a program that leaves them out, or rounds other values in their place, can miss the bound.
Values may be sent and summed in bfloat16 or wider, within the bound.
No kernel may reach another device: no remote copies, remote signals or barrier semaphores. Data moves between devices by JAX's collectives and lax.ppermute only.
A program may use at most 128 MiB of HBM per device.

v0:
```python
import math

import jax
import jax.numpy as jnp
from jax import lax
from jax.sharding import PartitionSpec as P

D = 3072
HD = 128
CH = 64
GRID_W = 128


epsilon = 1e-06
time_shift = 3.0


def in_blocks(x, dim, peers):
    lengths = x.shape
    tiles = x.reshape(*lengths[:dim], peers, lengths[dim] // peers, *lengths[dim + 1 :])
    return jnp.moveaxis(tiles, dim, 0)


def sent_and_summed(x, axis, dim):
    peers = lax.axis_size(axis)
    tiles = lax.all_to_all(in_blocks(x, dim, peers), axis, 0, 0, tiled=True)
    return jnp.sum(tiles.astype(jnp.float32), axis=0)


def swapped(x, axis, bit):
    return lax.ppermute(x, axis, [(i, i ^ 1 << bit) for i in range(lax.axis_size(axis))])


def layer_norm(values):
    mean_val = jnp.mean(values, axis=-1, keepdims=True)
    centered = values - mean_val
    variance = jnp.mean(centered * centered, axis=-1, keepdims=True)
    return centered * lax.rsqrt(variance + epsilon)


def rms_norm(values, gain_vec):
    return (
        values * lax.rsqrt(jnp.mean(values * values, axis=-1, keepdims=True) + epsilon) * gain_vec
    )


def rotate(values, positions, grid_width):
    quarter = values.shape[-1] // 4
    freqs = 10000.0 ** (-jnp.arange(quarter, dtype=jnp.float32) / quarter)
    row_pos = (positions // grid_width).astype(jnp.float32)
    col_pos = (positions % grid_width).astype(jnp.float32)
    angles = jnp.stack(
        [row_pos[:, None] * freqs[None, :], col_pos[:, None] * freqs[None, :]], axis=1
    )
    cosine = jnp.cos(angles)[:, None]
    sine = jnp.sin(angles)[:, None]
    shaped = values.reshape(values.shape[0], values.shape[1], 2, 2, quarter)
    first = shaped[:, :, :, 0]
    second = shaped[:, :, :, 1]
    turned = jnp.stack([first * cosine - second * sine, second * cosine + first * sine], axis=3)
    return turned.reshape(values.shape)


def noise_level(index, count):
    frac = 1.0 - index / count
    lift = math.exp(time_shift)
    return lift * frac / (lift * frac + 1.0 - frac)


def log_ratio(sigma_val):
    return jnp.log(1.0 - sigma_val) - jnp.log(sigma_val)


def solver_step(cond, uncond, guidance, step_index, step_count, latent, prev_denoised):
    guided = uncond + guidance[0] * (cond - uncond)
    index = step_index[0].astype(jnp.float32)
    count = step_count[0].astype(jnp.float32)
    sigma_prev = noise_level(index - 1.0, count)
    sigma_now = noise_level(index, count)
    sigma_next = noise_level(index + 1.0, count)
    step_now = log_ratio(sigma_next) - log_ratio(sigma_now)
    step_prev = log_ratio(sigma_now) - log_ratio(sigma_prev)
    ratio = step_prev / step_now
    denoised = latent - sigma_now * guided
    blend = (1.0 + 0.5 / ratio) * denoised - 0.5 / ratio * prev_denoised
    next_latent = (
        sigma_next / sigma_now * latent - (1.0 - sigma_next) * (jnp.exp(-step_now) - 1.0) * blend
    )
    return (next_latent, denoised)


def body(
    img_hidden,
    txt_hidden,
    modulation,
    w_qkv,
    q_gain,
    k_gain,
    w_out,
    b_out,
    stale_kv,
    final_mod,
    w_final,
    b_final,
    latent,
    prev_denoised,
    guidance,
    step_index,
    step_count,
):
    head_width = w_out.shape[0]
    head_count = head_width // HD
    img_rows = img_hidden.shape[1]
    txt_rows = txt_hidden.shape[1]
    kv_rows = img_rows + txt_rows
    out_rows = latent.shape[0]
    patch_index = lax.axis_index("patch")
    cfg_index = lax.axis_index("cfg")
    head_index = lax.axis_index("head")
    head_total = lax.axis_size("head")
    inv_root = HD ** (-0.5)
    shift_vec = modulation[0, 0]
    scale_vec = modulation[0, 1]
    gate_vec = modulation[0, 2]
    modded_img = (
        layer_norm(img_hidden[0].astype(jnp.float32)) * (1.0 + scale_vec) + shift_vec
    ).astype(jnp.bfloat16)
    modded_txt = (
        layer_norm(txt_hidden[0].astype(jnp.float32)) * (1.0 + scale_vec) + shift_vec
    ).astype(jnp.bfloat16)
    weight_flat = w_qkv.reshape(D, 3 * head_width)
    proj_img = jnp.dot(modded_img, weight_flat, preferred_element_type=jnp.float32).reshape(
        img_rows, 3, head_count, HD
    )
    proj_txt = jnp.dot(modded_txt, weight_flat, preferred_element_type=jnp.float32).reshape(
        txt_rows, 3, head_count, HD
    )
    positions = patch_index * img_rows + jnp.arange(img_rows, dtype=jnp.int32)
    queries = rotate(rms_norm(proj_img[:, 0], q_gain), positions, GRID_W).astype(jnp.bfloat16)
    img_keys = rotate(rms_norm(proj_img[:, 1], k_gain), positions, GRID_W).astype(jnp.bfloat16)
    img_vals = proj_img[:, 2].astype(jnp.bfloat16)
    txt_keys = rms_norm(proj_txt[:, 1], k_gain).astype(jnp.bfloat16)
    txt_vals = proj_txt[:, 2].astype(jnp.bfloat16)
    fresh_keys = jnp.concatenate([txt_keys, img_keys], axis=0)
    fresh_vals = jnp.concatenate([txt_vals, img_vals], axis=0)
    fresh_kv = jnp.stack(
        [fresh_keys.reshape(kv_rows, head_width), fresh_vals.reshape(kv_rows, head_width)]
    )[None]

    def scores_of(key_block):
        return (
            jnp.einsum("qhd,khd->hqk", queries, key_block, preferred_element_type=jnp.float32)
            * inv_root
        )

    own_scores = scores_of(fresh_keys)
    own_top = jnp.max(own_scores, axis=-1)
    own_expo = jnp.exp(own_scores - own_top[..., None])
    own_total = jnp.sum(own_expo, axis=-1)
    own_acc = jnp.einsum(
        "hqk,khd->hqd",
        own_expo.astype(jnp.bfloat16),
        fresh_vals,
        preferred_element_type=jnp.float32,
    )
    own_first = patch_index * kv_rows
    block_piece = lax.all_gather(stale_kv, "patch", axis=2, tiled=True)
    key_count = block_piece.shape[2]
    key_block = block_piece[0, 0].reshape(key_count, head_count, HD)
    val_block = block_piece[0, 1].reshape(key_count, head_count, HD)
    scores = scores_of(key_block)
    row_ids = jnp.arange(key_count, dtype=jnp.int32)
    mine = (row_ids >= own_first) & (row_ids < own_first + kv_rows)
    scores = jnp.where(mine[None, None, :], -1e30, scores)
    top_new = jnp.maximum(own_top, jnp.max(scores, axis=-1))
    factor = jnp.exp(own_top - top_new)
    expo = jnp.exp(scores - top_new[..., None])
    total_new = own_total * factor + jnp.sum(expo, axis=-1)
    acc_new = own_acc * factor[..., None] + jnp.einsum(
        "hqk,khd->hqd", expo.astype(jnp.bfloat16), val_block, preferred_element_type=jnp.float32
    )
    attn = (
        (acc_new / total_new[..., None])
        .transpose(1, 0, 2)
        .reshape(img_rows, head_width)
        .astype(jnp.bfloat16)
    )
    hidden_in = img_hidden[0]
    ordered_attn = (
        attn.reshape(2, head_total, out_rows, head_width)
        .transpose(1, 0, 2, 3)
        .reshape(img_rows, head_width)
    )
    projected = sent_and_summed(
        jnp.dot(ordered_attn, w_out, preferred_element_type=jnp.float32).astype(jnp.bfloat16),
        "head",
        0,
    )
    own_hidden = lax.dynamic_index_in_dim(
        hidden_in.reshape(2, head_total, out_rows, D), head_index, 1, keepdims=False
    ).reshape(2 * out_rows, D)
    mixed = own_hidden.astype(jnp.float32) + gate_vec * (projected + b_out)
    final_in = (layer_norm(mixed) * (1.0 + final_mod[0, 1]) + final_mod[0, 0]).astype(jnp.bfloat16)
    velocity = (jnp.dot(final_in, w_final, preferred_element_type=jnp.float32) + b_final).reshape(
        2, out_rows, CH
    )
    partner = swapped(velocity, "cfg", 0)
    own_rows = lax.dynamic_index_in_dim(velocity, cfg_index, 0, keepdims=False)
    partner_rows = lax.dynamic_index_in_dim(partner, cfg_index, 0, keepdims=False)
    cond = jnp.where(cfg_index == 0, own_rows, partner_rows)
    uncond = jnp.where(cfg_index == 0, partner_rows, own_rows)
    next_latent, denoised = solver_step(
        cond, uncond, guidance, step_index, step_count, latent, prev_denoised
    )
    return (fresh_kv, next_latent, denoised)


def solution(mesh):
    return jax.shard_map(
        body,
        mesh=mesh,
        in_specs=(
            P("cfg", ("groups", "patch"), None),
            P("cfg", ("groups", "patch"), None),
            P(("groups", "cfg"), None, None),
            P(None, None, "head"),
            P(),
            P(),
            P("head", None),
            P(),
            P("cfg", None, ("groups", "patch"), "head"),
            P(("groups", "cfg"), None, None),
            P(),
            P(),
            P(("groups", "patch", "cfg", "head"), None),
            P(("groups", "patch", "cfg", "head"), None),
            P("groups"),
            P(),
            P(),
        ),
        out_specs=(
            P("cfg", None, ("groups", "patch"), "head"),
            P(("groups", "patch", "cfg", "head"), None),
            P(("groups", "patch", "cfg", "head"), None),
        ),
        check_vma=False,
    )
```

profile of v0, /device:TPU:33, one launch (start us, length us, event | category | flops | bytes accessed | tf_op | source)
XLA Modules:
  0.0 220.0 jit_solution(4321389743603134770)
XLA Ops:
  7.2 0.0 copy-start
  7.2 0.1 all-gather.2.cloned.1.call-start
  7.3 2.2 %copy.56 = bf16[1,2,272,384]{3,1,0,2:T(2,128)(2,1)} copy(bf16[1,2,272,384]{3,2,1,0:T(8,128)(2,1)} %param.25) | data formatting | bytes 835584 | tf_op args[8]
  9.5 0.1 all-gather.2.cloned.1.call-update
  9.6 0.0 copy-start.5
  9.6 0.0 copy-start.12
  9.6 10.1 %copy.46 = bf16[3072,3,384]{0,2,1:T(8,128)(2,1)} copy(bf16[3072,3,384]{2,0,1:T(8,128)(2,1)} %param.20) | data formatting | bytes 14155776 | tf_op args[3]
  19.7 0.1 convert_reduce_fusion.2
  19.9 0.2 fusion.49
  20.2 5.0 %fusion.51 = f32[16,3,3,128]{3,0,2,1:T(8,128)S(1)} fusion(bf16[3,3,128,3072]{3,2,1,0:T(8,128)(2,1)} %bitcast.140, bf16[1,16,3072]{2,1,0:T(8,128)(2,1)S(1)} %copy-done.5, f32[3072]{0:T(1024)S(1)} %bitcast.169, f32[3072]{0:T(1024)S(1)} %bitcast.167, f32[16]{0:T(128)S(1)} %add_rsqrt_fusion.5, f32[16]{0:T(128)S(1)} %broadcast_multiply_fusion.4), kind=kOutput, calls=%fused_computation.76 | convolution fusion | flops 113541120 | bytes 7274624 | tf_op jit(solution)/shard_map/dot_general | solution.py:135
  25.2 0.7 mul.433
  25.8 0.1 mul.404
  25.9 0.1 fusion.59
  26.0 0.1 copy.77
  26.1 0.6 squeeze.14
  26.7 0.1 mul.389.clone
  26.8 0.6 mul.390
  27.5 0.8 copy.54
  28.2 1.7 convert_reduce_fusion
  29.9 2.0 fusion.12
  31.9 5.7 %fusion.14 = f32[256,3,3,128]{0,3,2,1:T(8,128)S(1)} fusion(bf16[3,3,128,3072]{3,2,1,0:T(8,128)(2,1)} %bitcast.141, bf16[1,256,3072]{2,1,0:T(8,128)(2,1)} %param.17, f32[3072]{0:T(1024)S(1)} %bitcast.170, f32[3072]{0:T(1024)S(1)} %bitcast.168, f32[256]{0:T(256)S(1)} %add_rsqrt_fusion.4, f32[256]{0:T(256)S(1)} %broadcast_multiply_fusion.3), kind=kOutput, calls=%fused_computation.20 | convolution fusion | flops 1816657920 | bytes 9857024 | tf_op jit(solution)/shard_map/dot_general | solution.py:132
  37.6 0.8 slice.91
  38.4 0.1 broadcast_multiply_fusion.1
  38.5 0.2 fusion.58
  38.7 0.1 multiply_reduce_fusion.1
  38.9 0.1 multiply_multiply_fusion.1
  39.0 0.1 multiply_subtract_fusion
  39.1 0.8 copy.52
  39.9 0.8 multiply_multiply_fusion
  40.7 0.1 subtract_convert_fusion
  40.8 0.8 fusion.61
  41.6 1.2 fusion.79
  42.8 0.9 copy-done.2
  43.7 0.1 fusion.32
  43.9 1.7 slice_bitcast_fusion.1
  45.6 65.8 %all-gather.2.cloned.1.call-done = bf16[1,2,4352,384]{3,1,0,2:T(2,128)(2,1)} async-done(((bf16[1,2,272,384]{3,1,0,2:T(2,128)(2,1)}), bf16[1,2,4352,384]{3,1,0,2:T(2,128)(2,1)}) %all-gather.2.cloned.1.call-update) | async-done | bytes 6684688 | tf_op jit(solution)/shard_map/all_gather | solution.py:167
  111.4 14.7 %fusion.77 = (bf16[1,1,4352,384]{3,1,0,2:T(2,128)(2,1)}, bf16[1,1,4352,384]{3,1,0,2:T(2,128)(2,1)}) fusion(bf16[1,2,4352,384]{3,1,0,2:T(2,128)(2,1)} %all-gather.2.cloned.1.call-done), kind=kLoop, calls=%fused_computation.133 | loop fusion | bytes 13369344 | tf_op jit(solution)/shard_map/slice | solution.py:169
  126.2 14.2 %copy.75 = bf16[1,1,4352,384]{2,3,1,0:T(8,128)(2,1)} copy(bf16[1,1,4352,384]{3,1,0,2:T(2,128)(2,1)} %get-tuple-element.15) | data formatting | bytes 6684672
  140.3 14.2 %copy.76 = bf16[1,1,4352,384]{2,3,1,0:T(8,128)(2,1)} copy(bf16[1,1,4352,384]{3,1,0,2:T(2,128)(2,1)} %get-tuple-element.16) | data formatting | bytes 6684672
  154.6 4.3 %fusion = (f32[3,256]{1,0:T(4,128)S(1)}, f32[3,256,4352]{2,1,0:T(8,128)S(1)}) fusion(pred[4352]{0:T(1024)(128)(4,1)S(1)} %fusion.62, bf16[256,3,128]{0,2,1:T(8,128)(2,1)S(1)} %bitcast.151, bf16[4352,3,128]{0,2,1:T(8,128)(2,1)} %bitcast.142), kind=kOutput, calls=%fused_computation.2 | convolution fusion | flops 865664256 | bytes 16915712 | tf_op jit(solution)/shard_map/qhd,khd->hqk/dot_general | solution.py:152
  158.8 3.0 %fusion.1 = f32[3,256]{1,0:T(4,128)S(1)} fusion(f32[3,256,4352]{2,1,0:T(8,128)S(1)} %get-tuple-element.34, f32[3,256]{1,0:T(4,128)S(1)} %max.18, pred[4352]{0:T(1024)(128)(4,1)S(1)} %fusion.62), kind=kLoop, calls=%fused_computation.3 | loop fusion | flops 13368576 | bytes 13379840 | tf_op jit(solution)/shard_map/reduce_sum | solution.py:178
  161.8 1.8 copy-done.1
  163.6 7.4 %fusion.20 = f32[256,3,128]{2,0,1:T(8,128)S(1)} fusion(bf16[4352,3,128]{0,2,1:T(8,128)(2,1)} %bitcast.149, f32[3,256,4352]{2,1,0:T(8,128)} %copy-done.1, f32[3,256]{1,0:T(4,128)S(1)} %max.18, pred[4352]{0:T(1024)(128)(4,1)S(1)} %fusion.62), kind=kOutput, calls=%fused_computation.26 | convolution fusion | flops 869007360 | bytes 17112320 | tf_op jit(solution)/shard_map/hqk,khd->hqd/dot_general | solution.py:179
  171.0 0.6 fusion.26
  171.6 0.2 copy.62
  171.8 0.2 convert_element_type.181
  172.0 0.0 copy-start.13
  172.0 2.1 convolution_convert_fusion
  174.2 4.6 %all-to-all-start = ((bf16[4,64,3072]{2,1,0:T(8,128)(2,1)}), bf16[4,64,3072]{2,1,0:T(8,128)(2,1)}, u32[]{:S(2)}, u32[]{:S(2)}) async-start(bf16[4,64,3072]{2,1,0:T(8,128)(2,1)} %bitcast.148), calls=%async_computation | async-start | bytes 3145728 | tf_op jit(solution)/shard_map/all_to_all | solution.py:26
  178.8 0.1 copy.49
  178.9 0.8 copy.72
  179.7 1.9 dynamic-slice_convert_fusion
  181.6 16.5 %all-to-all-done = bf16[4,64,3072]{2,1,0:T(8,128)(2,1)} async-done(((bf16[4,64,3072]{2,1,0:T(8,128)(2,1)}), bf16[4,64,3072]{2,1,0:T(8,128)(2,1)}, u32[]{:S(2)}, u32[]{:S(2)}) %all-to-all-start) | async-done | bytes 1572896 | tf_op jit(solution)/shard_map/all_to_all | solution.py:26
  198.2 1.7 convert_reduce_fusion.1
  199.9 1.2 fusion.39
  201.2 1.3 multiply_reduce_fusion
  202.5 0.1 div.111
  202.6 0.1 rsqrt.57
  202.6 1.4 fusion.31
  204.0 1.2 convolution_add_fusion
  205.3 2.3 %collective-permute-start = (f32[2,32,64]{2,1,0:T(8,128)S(1)}, f32[2,32,64]{2,1,0:T(8,128)S(1)}, u32[]{:S(2)}, u32[]{:S(2)}) collective-permute-start(f32[2,32,64]{2,1,0:T(8,128)S(1)} %bitcast.163), channel_id=1, source_target_pairs={{0,4},{4,0},{1,5},{5,1},{2,6},{6,2},{3,7},{7,3},{8,12},{12,8},{9,1... | collective-permute-start | bytes 49160 | tf_op jit(solution)/shard_map/ppermute | solution.py:31
  207.6 1.3 maximum_bitcast_fusion
  211.4 1.0 copy.64
  212.5 0.6 multiply_subtract_fusion.1
  (60 shorter events, 0.3 us)
Async XLA Ops:
  7.2 164.8 %copy-start = (bf16[384,3072]{1,0:T(8,128)(2,1)S(1)}, bf16[384,3072]{1,0:T(8,128)(2,1)}, u32[]{:S(2)}) copy-start(bf16[384,3072]{1,0:T(8,128)(2,1)} %param.23) | copy-start | bytes 7077892
  7.2 104.2 %all-gather.2.cloned.1.call-start = ((), (), s32[]{:S(2)}) async-start(), calls=%async_computation.1 | async-start | bytes 7102464 | tf_op jit(solution)/shard_map/all_gather | solution.py:167
  9.6 10.2 %copy-start.5 = (bf16[1,16,3072]{2,1,0:T(8,128)(2,1)S(1)}, bf16[1,16,3072]{2,1,0:T(8,128)(2,1)}, u32[]{:S(2)}) copy-start(bf16[1,16,3072]{2,1,0:T(8,128)(2,1)} %param.18) | copy-start | bytes 294916
  9.6 10.5 %copy-start.12 = (f32[1,3,3072]{2,0,1:T(1,128)S(1)}, f32[1,3,3072]{2,0,1:T(1,128)}, u32[]{:S(2)}) copy-start(f32[1,3,3072]{2,0,1:T(1,128)} %param.19) | copy-start | bytes 110596
  20.1 5.0 %copy-start.18 = (f32[128]{0:T(128)S(1)}, f32[128]{0:T(128)}, u32[]{:S(2)}) copy-start(f32[128]{0:T(128)} %param.21) | copy-start | bytes 1540
  20.1 5.7 %copy-start.16 = (f32[128]{0:T(128)S(1)}, f32[128]{0:T(128)}, u32[]{:S(2)}) copy-start(f32[128]{0:T(128)} %param.22) | copy-start | bytes 1540
  25.1 12.5 %copy-start.6 = (f32[16,3,3,128]{3,0,2,1:T(8,128)}, f32[16,3,3,128]{3,0,2,1:T(8,128)S(1)}, u32[]{:S(2)}) copy-start(f32[16,3,3,128]{3,0,2,1:T(8,128)S(1)} %fusion.51) | copy-start | bytes 221188
  37.6 1.4 copy-start.4
  38.8 5.0 %copy-start.17 = (f32[128]{0:T(128)S(1)}, f32[128]{0:T(128)}, u32[]{:S(2)}) copy-start(f32[128]{0:T(128)} %param.22) | copy-start | bytes 1540
  42.8 0.9 copy-start.2
  158.8 4.7 %copy-start.1 = (f32[3,256,4352]{2,1,0:T(8,128)}, f32[3,256,4352]{2,1,0:T(8,128)S(1)}, u32[]{:S(2)}) copy-start(f32[3,256,4352]{2,1,0:T(8,128)S(1)} %get-tuple-element.34) | copy-start | bytes 40108036
  163.5 7.4 %copy-start.3 = (f32[3,256,272]{1,2,0:T(8,128)S(1)}, f32[3,256,272]{1,2,0:T(8,128)}, u32[]{:S(2)}) copy-start(f32[3,256,272]{1,2,0:T(8,128)} %copy-done.2) | copy-start | bytes 2506756
  163.6 7.4 %copy-start.7 = (bf16[256,3,128]{0,2,1:T(8,128)(2,1)S(1)}, bf16[256,3,128]{0,2,1:T(8,128)(2,1)}, u32[]{:S(2)}) copy-start(bf16[256,3,128]{0,2,1:T(8,128)(2,1)} %slice_bitcast_fusion.1) | copy-start | bytes 589828
  163.6 7.4 %copy-start.9 = (bf16[16,3,128]{0,2,1:T(8,128)(2,1)S(1)}, bf16[16,3,128]{0,2,1:T(8,128)(2,1)}, u32[]{:S(2)}) copy-start(bf16[16,3,128]{0,2,1:T(8,128)(2,1)} %copy.54) | copy-start | bytes 36868
  172.0 6.7 %copy-start.10 = (f32[1,16,384]{2,1,0:T(8,128)S(1)}, f32[1,16,384]{2,1,0:T(8,128)}, u32[]{:S(2)}) copy-start(f32[1,16,384]{2,1,0:T(8,128)} %squeeze.14) | copy-start | bytes 73732
  172.0 6.7 %copy-start.11 = (f32[1,16,384]{2,1,0:T(8,128)S(1)}, f32[1,16,384]{2,1,0:T(8,128)}, u32[]{:S(2)}) copy-start(f32[1,16,384]{2,1,0:T(8,128)} %mul.390) | copy-start | bytes 73732
  172.0 9.6 %copy-start.13 = (f32[1,2,3072]{2,1,0:T(2,128)S(1)}, f32[1,2,3072]{2,1,0:T(2,128)}, u32[]{:S(2)}) copy-start(f32[1,2,3072]{2,1,0:T(2,128)} %param.26) | copy-start | bytes 73732
  174.2 25.7 %copy-start.8 = (f32[3072]{0:T(1024)S(1)}, f32[3072]{0:T(1024)}, u32[]{:S(2)}) copy-start(f32[3072]{0:T(1024)} %param.24) | copy-start | bytes 36868
  174.2 24.0 %all-to-all-start = ((bf16[4,64,3072]{2,1,0:T(8,128)(2,1)}), bf16[4,64,3072]{2,1,0:T(8,128)(2,1)}, u32[]{:S(2)}, u32[]{:S(2)}) async-start(bf16[4,64,3072]{2,1,0:T(8,128)(2,1)} %bitcast.148), calls=%async_computation | async-start | bytes 3145728 | tf_op jit(solution)/shard_map/all_to_all | solution.py:26
  181.6 22.4 %copy-start.19 = (f32[64]{0:T(128)S(1)}, f32[64]{0:T(128)}, u32[]{:S(2)}) copy-start(f32[64]{0:T(128)} %param.28) | copy-start | bytes 772
  201.2 11.3 %copy-start.14 = (f32[32,64]{1,0:T(8,128)S(1)}, f32[32,64]{1,0:T(8,128)}, u32[]{:S(2)}) copy-start(f32[32,64]{1,0:T(8,128)} %param.30) | copy-start | bytes 24580
  201.2 11.3 %copy-start.15 = (f32[32,64]{1,0:T(8,128)S(1)}, f32[32,64]{1,0:T(8,128)}, u32[]{:S(2)}) copy-start(f32[32,64]{1,0:T(8,128)} %param.29) | copy-start | bytes 24580
  205.3 7.2 %collective-permute-start = (f32[2,32,64]{2,1,0:T(8,128)S(1)}, f32[2,32,64]{2,1,0:T(8,128)S(1)}, u32[]{:S(2)}, u32[]{:S(2)}) collective-permute-start(f32[2,32,64]{2,1,0:T(8,128)S(1)} %bitcast.163), channel_id=1, source_target_pairs={{0,4},{4,0},{1,5},{5,1},{2,6},{6,2},{3,7},{7,3},{8,12},{12,8},{9,1... | collective-permute-start | bytes 49160 | tf_op jit(solution)/shard_map/ppermute | solution.py:31
Sparse Core Ops, SparseCore 0:
  10.4 100.9 all-gather.1
where the time goes:
time: 222 us; the launch traced here: 220 us
  waiting for transfers between devices  82.4 us (37%)
  local copies, waits for them, and re-layouts  66.9 us (30%)
  matrix products  27.5 us (12%)
  other arithmetic  19.1 us (9%)
  between operations  17.1 us (8%)
  starting transfers between devices  6.96 us (3%)
    all_gather x1, waiting for transfers between devices, body(): block_piece = lax.all_gather(stale_kv, 'patch', axis=2, tiled=True)  65.8 us
    unnamed x46, local copies, waits for them, and re-layouts  44.6 us
    all_to_all x1, waiting for transfers between devices, sent_and_summed(): tiles = lax.all_to_all(in_blocks(x, dim, peers), axis, 0, 0, tiled=True)  16.5 us
    slice x1, local copies, waits for them, and re-layouts, body(): key_block = block_piece[0, 0].reshape(key_count, head_count, HD)  14.7 us
    dot_general x1, matrix products, body(): jnp.einsum('hqk,khd->hqd', expo.astype(jnp.bfloat16), val_block, preferre...  7.36 us
    dot_general x1, matrix products, body(): jnp.dot(modded_img, weight_flat, preferred_element_type=jnp.float32)  5.72 us
    dot_general x2, matrix products, scores_of(): jnp.einsum('qhd,khd->hqk', queries, key_block, preferred_element_type=jnp...  5.46 us
    dot_general x1, matrix products, body(): jnp.dot(modded_txt, weight_flat, preferred_element_type=jnp.float32)  4.95 us
  transfers between devices with their start and end apart: 3, of which 2 were waited for; matrix products, arithmetic and copies ran while one was open for 18% of the time, Pallas kernels for 0%

commit v1 on v0

v1 whole, which is shorter than its diff:
```python
import math

import jax
import jax.numpy as jnp
from jax import lax
from jax.experimental import pallas as pl
from jax.experimental.pallas import tpu as pltpu
from jax.sharding import PartitionSpec as P

D = 3072
HD = 128
CH = 64
GRID_W = 128


epsilon = 1e-06
time_shift = 3.0


def layer_norm(values):
    mean_val = jnp.mean(values, axis=-1, keepdims=True)
    centered = values - mean_val
    variance = jnp.mean(centered * centered, axis=-1, keepdims=True)
    return centered * lax.rsqrt(variance + epsilon)


def rms_norm(values, gain_vec):
    return (
        values * lax.rsqrt(jnp.mean(values * values, axis=-1, keepdims=True) + epsilon) * gain_vec
    )


def rotate(values, positions, grid_width):
    quarter = values.shape[-1] // 4
    freqs = 10000.0 ** (-jnp.arange(quarter, dtype=jnp.float32) / quarter)
    row_pos = (positions // grid_width).astype(jnp.float32)
    col_pos = (positions % grid_width).astype(jnp.float32)
    angles = jnp.stack(
        [row_pos[:, None] * freqs[None, :], col_pos[:, None] * freqs[None, :]], axis=1
    )
    cosine = jnp.cos(angles)[:, None]
    sine = jnp.sin(angles)[:, None]
    shaped = values.reshape(values.shape[0], values.shape[1], 2, 2, quarter)
    first = shaped[:, :, :, 0]
    second = shaped[:, :, :, 1]
    turned = jnp.stack([first * cosine - second * sine, second * cosine + first * sine], axis=3)
    return turned.reshape(values.shape)


def noise_level(index, count):
    frac = 1.0 - index / count
    lift = math.exp(time_shift)
    return lift * frac / (lift * frac + 1.0 - frac)


def log_ratio(sigma_val):
    return jnp.log(1.0 - sigma_val) - jnp.log(sigma_val)


def solver_scalars(guidance, step_index, step_count):
    index = step_index[0].astype(jnp.float32)
    count = step_count[0].astype(jnp.float32)
    sigma_prev = noise_level(index - 1.0, count)
    sigma_now = noise_level(index, count)
    sigma_next = noise_level(index + 1.0, count)
    step_now = log_ratio(sigma_next) - log_ratio(sigma_now)
    step_prev = log_ratio(sigma_now) - log_ratio(sigma_prev)
    ratio = step_prev / step_now
    return jnp.stack(
        [
            guidance[0],
            sigma_now,
            1.0 + 0.5 / ratio,
            0.5 / ratio,
            sigma_next / sigma_now,
            (1.0 - sigma_next) * (jnp.exp(-step_now) - 1.0),
        ]
    )


def attend_kernel(where, q_ref, fresh_ref, gathered_ref, out_ref, keys, vals, key_sem, val_sem):
    blocks, _, kv_rows, width = gathered_ref.shape
    heads = width // HD
    mine = where[0]
    for index, (held, sem) in enumerate(((keys, key_sem), (vals, val_sem))):
        for block in range(blocks):

            @pl.when(mine == block)
            def _():
                pltpu.make_async_copy(fresh_ref.at[index], held.at[block], sem.at[block]).start()

            @pl.when(mine != block)
            def _():
                pltpu.make_async_copy(
                    gathered_ref.at[block, index], held.at[block], sem.at[block]
                ).start()

    def arrived(held, sem):
        for block in range(blocks):
            pltpu.make_async_copy(fresh_ref.at[0], held.at[block], sem.at[block]).wait()

    scale = math.log2(math.e) * HD ** (-0.5)
    total_keys = blocks * kv_rows
    arrived(keys, key_sem)
    for head in range(heads):
        lanes = pl.ds(head * HD, HD)
        key_mat = keys[:, :, lanes].reshape(total_keys, HD)
        scores = lax.dot_general(
            q_ref[:, lanes], key_mat, (((1,), (1,)), ((), ())), preferred_element_type=jnp.float32
        )
        top = jnp.max(scores, axis=-1, keepdims=True)
        expo = jnp.exp2(scores * scale - top * scale)
        denom = jnp.sum(expo, axis=-1, keepdims=True)
        if head == 0:
            arrived(vals, val_sem)
        val_mat = vals[:, :, lanes].reshape(total_keys, HD)
        acc = jnp.dot(expo.astype(jnp.bfloat16), val_mat, preferred_element_type=jnp.float32)
        out_ref[:, lanes] = (acc / denom).astype(jnp.bfloat16)


def attend(queries, fresh, gathered, patch_index):
    rows, width = queries.shape
    blocks, _, kv_rows, _ = gathered.shape
    flops = 4 * rows * blocks * kv_rows * width
    vmem = pl.BlockSpec(memory_space=pltpu.VMEM)
    hbm = pl.BlockSpec(memory_space=pl.ANY)
    return pl.pallas_call(
        attend_kernel,
        out_shape=jax.ShapeDtypeStruct((rows, width), jnp.bfloat16),
        in_specs=[pl.BlockSpec(memory_space=pltpu.SMEM), vmem, hbm, hbm],
        out_specs=vmem,
        scratch_shapes=[
            pltpu.VMEM((blocks, kv_rows, width), jnp.bfloat16),
            pltpu.VMEM((blocks, kv_rows, width), jnp.bfloat16),
            pltpu.SemaphoreType.DMA((blocks,)),
            pltpu.SemaphoreType.DMA((blocks,)),
        ],
        compiler_params=pltpu.CompilerParams(vmem_limit_bytes=40 * 1024 * 1024),
        cost_estimate=pl.CostEstimate(
            flops=flops,
            bytes_accessed=4 * blocks * kv_rows * width,
            transcendentals=rows * blocks * kv_rows * (width // HD),
        ),
        name="attend",
    )(patch_index.reshape(1), queries, fresh, gathered)


def finish_kernel(
    where,
    numbers,
    attn_ref,
    *refs,
):
    weights = refs[:4]
    (
        hidden_ref,
        gate_ref,
        shift_ref,
        scale_ref,
        b_out_ref,
        w_final_ref,
        b_final_ref,
        prev_ref,
        latent_ref,
        next_ref,
        denoised_ref,
    ) = refs[4:]
    rows = latent_ref.shape[0]
    here = where[0]
    peers = len(weights)

    def of_both(vec_ref):
        return jnp.concatenate(
            [jnp.broadcast_to(vec_ref[b], (rows, vec_ref.shape[-1])) for b in range(2)], axis=0
        )

    projected = None
    for shift, w_ref in enumerate(weights):
        source = lax.rem(here + peers - shift, peers)
        left = jnp.concatenate([attn_ref[b, source] for b in range(2)], axis=0)
        term = jnp.dot(left, w_ref[...], preferred_element_type=jnp.float32)
        projected = term if projected is None else projected + term
    mixed = hidden_ref[...].astype(jnp.float32) + of_both(gate_ref) * (projected + b_out_ref[...])
    normed = layer_norm(mixed)
    final_in = (normed * (1.0 + of_both(scale_ref)) + of_both(shift_ref)).astype(jnp.bfloat16)
    velocity = (
        jnp.dot(final_in, w_final_ref[...], preferred_element_type=jnp.float32) + b_final_ref[...]
    )
    cond = velocity[:rows]
    uncond = velocity[rows:]
    guided = uncond + numbers[0] * (cond - uncond)
    latent = latent_ref[...]
    denoised = latent - numbers[1] * guided
    blend = numbers[2] * denoised - numbers[3] * prev_ref[...]
    denoised_ref[...] = denoised
    next_ref[...] = numbers[4] * latent - numbers[5] * blend


def finish(where, numbers, attn, weights, *rest):
    latent = rest[-1]
    out = jax.ShapeDtypeStruct(latent.shape, jnp.float32)
    smem = pl.BlockSpec(memory_space=pltpu.SMEM)
    vmem = pl.BlockSpec(memory_space=pltpu.VMEM)
    depth = sum(w.shape[0] for w in weights)
    return pl.pallas_call(
        finish_kernel,
        out_shape=(out, out),
        in_specs=[smem, smem] + [vmem] * (1 + len(weights) + len(rest)),
        out_specs=(vmem, vmem),
        compiler_params=pltpu.CompilerParams(vmem_limit_bytes=40 * 1024 * 1024),
        cost_estimate=pl.CostEstimate(
            flops=4 * latent.shape[0] * depth * D,
            bytes_accessed=2 * depth * D,
            transcendentals=0,
        ),
        name="finish",
    )(where, numbers, attn, *weights, *rest)


def body(
    img_hidden,
    txt_hidden,
    modulation,
    w_qkv,
    q_gain,
    k_gain,
    w_out,
    b_out,
    stale_kv,
    final_mod,
    w_final,
    b_final,
    latent,
    prev_denoised,
    guidance,
    step_index,
    step_count,
):
    head_width = w_out.shape[0]
    head_count = head_width // HD
    img_rows = img_hidden.shape[1]
    txt_rows = txt_hidden.shape[1]
    kv_rows = img_rows + txt_rows
    out_rows = latent.shape[0]
    patch_index = lax.axis_index("patch")
    cfg_index = lax.axis_index("cfg")
    head_index = lax.axis_index("head")
    head_total = lax.axis_size("head")

    gathered = lax.all_gather(
        stale_kv.reshape(2 * kv_rows, head_width), "patch", axis=0, tiled=False
    ).reshape(-1, 2, kv_rows, head_width)

    weights = [w_out] + [
        lax.ppermute(w_out, "head", [(i, (i + shift) % head_total) for i in range(head_total)])
        for shift in range(1, head_total)
    ]
    swap = [(0, 1), (1, 0)]
    hidden_rows = img_hidden.reshape(2, head_total, out_rows, D)
    hidden_mine = lax.dynamic_index_in_dim(hidden_rows, head_index, 1, keepdims=False)
    own_hidden = lax.dynamic_index_in_dim(hidden_mine, cfg_index, 0, keepdims=False)
    sent_hidden = lax.dynamic_index_in_dim(hidden_mine, 1 - cfg_index, 0, keepdims=False)
    other_hidden = lax.ppermute(sent_hidden, "cfg", swap)
    own_vecs = jnp.concatenate([modulation[0, 2:], final_mod[0]], axis=0)
    other_vecs = lax.ppermute(own_vecs, "cfg", swap)
    first = cfg_index == 0
    hidden = jnp.concatenate(
        [
            jnp.where(first, own_hidden, other_hidden),
            jnp.where(first, other_hidden, own_hidden),
        ],
        axis=0,
    )
    vecs = jnp.stack(
        [jnp.where(first, own_vecs, other_vecs), jnp.where(first, other_vecs, own_vecs)], axis=0
    )
    numbers = solver_scalars(guidance, step_index, step_count)

    shift_vec = modulation[0, 0]
    scale_vec = modulation[0, 1]
    modded_img = (
        layer_norm(img_hidden[0].astype(jnp.float32)) * (1.0 + scale_vec) + shift_vec
    ).astype(jnp.bfloat16)
    modded_txt = (
        layer_norm(txt_hidden[0].astype(jnp.float32)) * (1.0 + scale_vec) + shift_vec
    ).astype(jnp.bfloat16)
    weight_flat = w_qkv.reshape(D, 3 * head_width)
    proj_img = jnp.dot(modded_img, weight_flat, preferred_element_type=jnp.float32).reshape(
        img_rows, 3, head_count, HD
    )
    proj_txt = jnp.dot(modded_txt, weight_flat, preferred_element_type=jnp.float32).reshape(
        txt_rows, 3, head_count, HD
    )
    positions = patch_index * img_rows + jnp.arange(img_rows, dtype=jnp.int32)
    queries = rotate(rms_norm(proj_img[:, 0], q_gain), positions, GRID_W).astype(jnp.bfloat16)
    img_keys = rotate(rms_norm(proj_img[:, 1], k_gain), positions, GRID_W).astype(jnp.bfloat16)
    img_vals = proj_img[:, 2].astype(jnp.bfloat16)
    txt_keys = rms_norm(proj_txt[:, 1], k_gain).astype(jnp.bfloat16)
    txt_vals = proj_txt[:, 2].astype(jnp.bfloat16)
    fresh_keys = jnp.concatenate([txt_keys, img_keys], axis=0)
    fresh_vals = jnp.concatenate([txt_vals, img_vals], axis=0)
    fresh_kv = jnp.stack(
        [fresh_keys.reshape(kv_rows, head_width), fresh_vals.reshape(kv_rows, head_width)]
    )

    attn = attend(queries.reshape(img_rows, head_width), fresh_kv, gathered, patch_index)
    shared = lax.all_to_all(
        attn.reshape(2 * head_total, out_rows, head_width), ("cfg", "head"), 0, 0, tiled=True
    ).reshape(2, head_total, out_rows, head_width)
    next_latent, denoised = finish(
        head_index.reshape(1),
        numbers,
        shared,
        weights,
        hidden,
        vecs[:, 0:1],
        vecs[:, 1:2],
        vecs[:, 2:3],
        b_out.reshape(1, D),
        w_final,
        b_final.reshape(1, CH),
        prev_denoised,
        latent,
    )
    return (fresh_kv[None], next_latent, denoised)


def solution(mesh):
    return jax.shard_map(
        body,
        mesh=mesh,
        in_specs=(
            P("cfg", ("groups", "patch"), None),
            P("cfg", ("groups", "patch"), None),
            P(("groups", "cfg"), None, None),
            P(None, None, "head"),
            P(),
            P(),
            P("head", None),
            P(),
            P("cfg", None, ("groups", "patch"), "head"),
            P(("groups", "cfg"), None, None),
            P(),
            P(),
            P(("groups", "patch", "cfg", "head"), None),
            P(("groups", "patch", "cfg", "head"), None),
            P("groups"),
            P(),
            P(),
        ),
        out_specs=(
            P("cfg", None, ("groups", "patch"), "head"),
            P(("groups", "patch", "cfg", "head"), None),
            P(("groups", "patch", "cfg", "head"), None),
        ),
        check_vma=False,
    )
```

time: 222 us -> 162 us (0.73)
  local copies, waits for them, and re-layouts: 66.9 us -> 23 us
  waiting for transfers between devices: 82.4 us -> 48 us
  starting transfers between devices: 6.96 us -> 29.6 us
  Pallas kernels: 0 us -> 22.6 us
  matrix products: 27.5 us -> 10.3 us
  other arithmetic: 19.1 us -> 10.2 us
    unnamed x46 -> x38, local copies, waits for them, and re-layouts: 44.6 us -> 19.7 us
    all_gather x1, waiting for transfers between devices: 65.8 us -> 42.4 us  [body(): lax.all_gather(stale_kv.reshape(2 * kv_rows, head_width), 'patch', axis=0...]
    pallas_call x0 -> x2, Pallas kernels: none -> 22.6 us  [the longest x1 16.5 us: attend(): pl.pallas_call(attend_kernel, out_shape=jax.ShapeDtypeStruct((rows, width...]
    ppermute x1 -> x5, starting transfers between devices: 2.34 us -> 23.8 us  [the longest x1 17.7 us: body(): other_hidden = lax.ppermute(sent_hidden, 'cfg', swap)]
    dot_general x6 -> x0, matrix products: 16.8 us -> none  [the longest x1 7.36 us: body(): jnp.einsum('hqk,khd->hqd', expo.astype(jnp.bfloat16), val_block, preferre...]
    slice x2 -> x0, local copies, waits for them, and re-layouts: 14.7 us -> none  [the longest x1 14.7 us: body(): key_block = block_piece[0, 0].reshape(key_count, head_count, HD)]
    all_to_all x1, waiting for transfers between devices: 16.5 us -> 4.85 us  [body(): lax.all_to_all(attn.reshape(2 * head_total, out_rows, head_width), ('cfg'...]
    reduce_sum x3 -> x0, other arithmetic: 4.83 us -> none  [the longest x1 2.97 us: body(): total_new = own_total * factor + jnp.sum(expo, axis=-1)]
  transfers between devices with their start and end apart: 3 -> 7, of which waited for: 2 -> 2; matrix products, arithmetic and copies ran while one was open for 18% -> 22% of each run, Pallas kernels for 0% -> 10%
where the time goes in v1:
time: 162 us; the launch traced here: 161 us
  waiting for transfers between devices  48 us (30%)
  starting transfers between devices  29.6 us (18%)
  local copies, waits for them, and re-layouts  23 us (14%)
  Pallas kernels  22.6 us (14%)
  between operations  16.9 us (10%)
  matrix products  10.3 us (6%)
  other arithmetic  10.2 us (6%)
    all_gather x1, waiting for transfers between devices, body(): lax.all_gather(stale_kv.reshape(2 * kv_rows, head_width), 'patch', axis=0...  42.4 us
    unnamed x38, local copies, waits for them, and re-layouts  19.7 us
    ppermute x1, starting transfers between devices, body(): other_hidden = lax.ppermute(sent_hidden, 'cfg', swap)  17.7 us
    pallas_call x1, Pallas kernels, attend(): pl.pallas_call(attend_kernel, out_shape=jax.ShapeDtypeStruct((rows, width...  16.5 us
    pallas_call x1, Pallas kernels, finish(): pl.pallas_call(finish_kernel, out_shape=(out, out), in_specs=[smem, smem]...  6.11 us
    ppermute x3, starting transfers between devices, body(): lax.ppermute(w_out, 'head', [(i, (i + shift) % head_total) for i in range...  6.02 us
    all_to_all x1, starting transfers between devices, body(): lax.all_to_all(attn.reshape(2 * head_total, out_rows, head_width), ('cfg'...  5.81 us
    dot_general x1, matrix products, body(): jnp.dot(modded_img, weight_flat, preferred_element_type=jnp.float32)  5.29 us
  transfers between devices with their start and end apart: 7, of which 2 were waited for; matrix products, arithmetic and copies ran while one was open for 22% of the time, Pallas kernels for 10%

profile of v1, /device:TPU:33, one launch (start us, length us, event | category | flops | bytes accessed | tf_op | source)
XLA Modules:
  0.0 160.7 jit_solution(686366623027468634)
XLA Ops:
  7.2 0.1 all-gather.2.cloned.1.call-start
  7.2 0.7 all-gather.2.cloned.1.call-update
  8.0 2.3 %collective-permute-start = (bf16[384,3072]{1,0:T(8,128)(2,1)}, bf16[384,3072]{1,0:T(8,128)(2,1)}, u32[]{:S(2)}, u32[]{:S(2)}) collective-permute-start(bf16[384,3072]{1,0:T(8,128)(2,1)} %refs_0_.1), channel_id=1, source_target_pairs={{0,1},{1,2},{2,3},{3,0},{4,5},{5,6},{6,7},{7,4},{8,9},{9,10},{10,1... | collective-permute-start | bytes 7077896 | tf_op jit(solution)/shard_map/ppermute | solution.py:255
  10.2 2.7 %collective-permute-start.1 = (bf16[384,3072]{1,0:T(8,128)(2,1)}, bf16[384,3072]{1,0:T(8,128)(2,1)}, u32[]{:S(2)}, u32[]{:S(2)}) collective-permute-start(bf16[384,3072]{1,0:T(8,128)(2,1)} %refs_0_.1), channel_id=1, source_target_pairs={{0,2},{1,3},{2,0},{3,1},{4,6},{5,7},{6,4},{7,5},{8,10},{9,11},{10,... | collective-permute-start | bytes 7077896 | tf_op jit(solution)/shard_map/ppermute | solution.py:255
  13.0 1.0 collective-permute-start.2
  14.0 1.6 %dynamic-slice_bitcast_fusion = bf16[32,3072]{1,0:T(8,128)(2,1)} fusion(bf16[2,4,32,3072]{3,2,1,0:T(8,128)(2,1)} %bitcast.85, s32[]{:T(128)S(6)} %select_n.72, s32[]{:T(128)S(6)} %select_n.70), kind=kLoop, calls=%fused_computation.37 | loop fusion | bytes 393224 | tf_op jit(solution)/shard_map/jit(dynamic_index_in_dim)/squeeze | solution.py:262
  15.6 17.7 %collective-permute-start.3 = (bf16[32,3072]{1,0:T(8,128)(2,1)}, bf16[32,3072]{1,0:T(8,128)(2,1)}, u32[]{:S(2)}, u32[]{:S(2)}) collective-permute-start(bf16[32,3072]{1,0:T(8,128)(2,1)} %dynamic-slice_bitcast_fusion), channel_id=1, source_target_pairs={{0,4},{4,0},{1,5},{5,1},{2,6},{6,2},{3,7},{7,3},{8,12},{12,8},{9,1... | collective-permute-start | bytes 589832 | tf_op jit(solution)/shard_map/ppermute | solution.py:263
  33.4 0.8 slice_bitcast_fusion
  34.1 1.4 pad_maximum_fusion.4
  35.5 0.0 collective-permute-start.4
  35.5 10.4 %copy.33 = bf16[3072,3,384]{0,2,1:T(8,128)(2,1)} copy(bf16[3072,3,384]{2,0,1:T(8,128)(2,1)} %param.20) | data formatting | bytes 14155776 | tf_op args[3]
  45.9 0.0 copy-done.11
  45.9 0.3 convert_reduce_fusion
  46.2 0.6 fusion.6
  46.8 0.0 copy-start.12
  46.8 5.3 %fusion.8 = f32[256,3,3,128]{0,3,2,1:T(8,128)S(1)} fusion(bf16[3,3,128,3072]{3,2,1,0:T(8,128)(2,1)} %bitcast.83, bf16[1,256,3072]{2,1,0:T(8,128)(2,1)S(1)} %copy-done.11, f32[3072]{0:T(1024)S(1)} %bitcast.97, f32[3072]{0:T(1024)S(1)} %bitcast.95, f32[256]{0:T(256)S(1)} %add_rsqrt_fusion.3, f32[256]{0:T(256)S(1)} %broadcast_multiply_fusion.2), kind=kOutput, calls=%fused_computation.11 | convolution fusion | flops 1816657920 | bytes 9857024 | tf_op jit(solution)/shard_map/dot_general | solution.py:288
  52.1 0.2 copy.38
  52.3 0.1 convert_reduce_fusion.1
  52.5 0.2 fusion.20
  52.7 0.0 copy-start.17
  52.7 0.0 copy-start.16
  52.7 5.0 %fusion.22 = f32[16,3,3,128]{3,0,2,1:T(8,128)S(1)} fusion(bf16[3,3,128,3072]{3,2,1,0:T(8,128)(2,1)} %bitcast.84, bf16[1,16,3072]{2,1,0:T(8,128)(2,1)S(1)} %copy-done.12, f32[3072]{0:T(1024)S(1)} %bitcast.98, f32[3072]{0:T(1024)S(1)} %bitcast.96, f32[16]{0:T(128)S(1)} %add_rsqrt_fusion.4, f32[16]{0:T(128)S(1)} %broadcast_multiply_fusion.3), kind=kOutput, calls=%fused_computation.43 | convolution fusion | flops 113541120 | bytes 7274624 | tf_op jit(solution)/shard_map/dot_general | solution.py:291
  57.8 0.1 mul.311
  57.9 0.1 mul.289
  58.0 0.1 broadcast_multiply_fusion.1
  58.1 0.2 fusion.29
  58.3 0.1 multiply_reduce_fusion
  58.4 0.0 copy-start.13
  58.5 0.1 multiply_multiply_fusion
  58.6 0.0 copy-start.15
  58.6 0.1 multiply_multiply_fusion.1
  58.7 0.1 subtract_convert_fusion
  58.9 0.2 copy.36
  59.0 0.8 multiply_reduce_fusion.2
  59.9 0.1 copy.35
  60.0 0.1 mul.274
  60.1 1.0 maximum_maximum_fusion
  63.7 0.2 copy.39.q_ref
  63.8 0.4 copy.40.refs_9_
  64.3 0.7 stack.58.numbers
  65.0 0.0 collective-permute-done.4
  65.0 0.8 select_bitcast_fusion.1
  65.8 0.7 pad_maximum_fusion.5
  66.5 0.0 collective-permute-done.3
  66.5 1.7 %bitcast_select_fusion.1 = (bf16[32,3072]{1,0:T(8,128)(2,1)}, bf16[32,3072]{1,0:T(8,128)(2,1)}) fusion(bf16[32,3072]{1,0:T(8,128)(2,1)} %collective-permute-done.3, pred[]{:T(512)S(6)} %eq.6, bf16[2,4,32,3072]{3,2,1,0:T(8,128)(2,1)S(1)} %bitcast.86, s32[]{:T(128)S(6)} %select_n.68, s32[]{:T(128)S(6)} %select_n.70), kind=kLoop, calls=%fused_computation.36 | loop fusion | flops 196608 | bytes 786441 | tf_op jit(solution)/shard_map/jit(_where)/select_n | solution.py:269
  68.2 42.4 %all-gather.2.cloned.1.call-done = bf16[16,544,384]{2,1,0:T(8,128)(2,1)} async-done(((bf16[1,544,384]{2,1,0:T(8,128)(2,1)}), bf16[16,544,384]{2,1,0:T(8,128)(2,1)}) %all-gather.2.cloned.1.call-update) | async-done | bytes 6684688 | tf_op jit(solution)/shard_map/all_gather | solution.py:250
  110.6 2.9 %copy-done = bf16[16,544,384]{2,1,0:T(8,128)(2,1)S(1)} copy-done((bf16[16,544,384]{2,1,0:T(8,128)(2,1)S(1)}, bf16[16,544,384]{2,1,0:T(8,128)(2,1)}, u32[]{:S(2)}) %copy-start) | copy-done | bytes 6684696
  113.5 1.0 copy-done.2
  114.5 16.5 %attend.1 = bf16[256,384]{1,0:T(8,128)(2,1)} custom-call(s32[1]{0:T(128)} %bitcast.28.where, bf16[256,384]{1,0:T(8,128)(2,1)S(1)} %copy.39.q_ref, bf16[2,272,384]{2,1,0:T(8,128)(2,1)S(1)} %copy-done.2, bf16[16,2,272,384]{3,2,1,0:T(8,128)(2,1)S(1)} %bitcast.80), custom_call_target="tpu_custom_call" | custom-call | flops 1711276032 | bytes 6684672 | tf_op jit(solution)/shard_map/attend/pallas_call | solution.py:127
  131.1 5.8 %all-to-all-start = ((bf16[8,32,384]{2,1,0:T(8,128)(2,1)}), bf16[8,32,384]{2,1,0:T(8,128)(2,1)}, u32[]{:S(2)}, u32[]{:S(2)}) async-start(bf16[8,32,384]{2,1,0:T(8,128)(2,1)} %bitcast.33), calls=%async_computation | async-start | bytes 393216 | tf_op jit(solution)/shard_map/all_to_all | solution.py:307
  136.9 1.0 pad_maximum_fusion.refs_4_
  137.9 0.0 collective-permute-done.refs_1_
  137.9 0.0 collective-permute-done.1.refs_2_
  137.9 0.0 collective-permute-done.2.refs_3_
  137.9 4.8 %all-to-all-done = bf16[8,32,384]{2,1,0:T(8,128)(2,1)} async-done(((bf16[8,32,384]{2,1,0:T(8,128)(2,1)}), bf16[8,32,384]{2,1,0:T(8,128)(2,1)}, u32[]{:S(2)}, u32[]{:S(2)}) %all-to-all-start) | async-done | bytes 196640 | tf_op jit(solution)/shard_map/all_to_all | solution.py:307
  142.8 0.0 copy-done.6
  142.8 0.7 copy-done.3
  143.5 0.7 copy-done.4
  144.3 0.7 copy-done.5
  145.0 0.7 copy-done.7
  145.7 0.7 copy-done.8
  146.4 0.7 copy-done.9
  147.1 0.7 copy-done.10
  147.8 6.1 %finish.1 = (f32[32,64]{1,0:T(8,128)}, f32[32,64]{1,0:T(8,128)}) custom-call(s32[1]{0:T(128)} %bitcast.20.where, f32[6]{0:T(128)S(1)} %copy-done.9, bf16[2,4,32,384]{3,2,1,0:T(8,128)(2,1)} %bitcast.34.attn_ref, bf16[384,3072]{1,0:T(8,128)(2,1)S(1)} %copy-done.1, bf16[384,3072]{1,0:T(8,128)(2,1)} %collective-permute-done.refs_1_, ...), custom_call_target="tpu_custom_call" | custom-call | flops 603979776 | bytes 9437184 | tf_op jit(solution)/shard_map/finish/pallas_call | solution.py:205
  (39 shorter events, 0.3 us)
Async XLA Ops:
  7.2 103.4 %all-gather.2.cloned.1.call-start = ((), (), s32[]{:S(2)}) async-start(), calls=%async_computation.1 | async-start | bytes 7102464 | tf_op jit(solution)/shard_map/all_gather | solution.py:250
  8.0 129.9 %collective-permute-start = (bf16[384,3072]{1,0:T(8,128)(2,1)}, bf16[384,3072]{1,0:T(8,128)(2,1)}, u32[]{:S(2)}, u32[]{:S(2)}) collective-permute-start(bf16[384,3072]{1,0:T(8,128)(2,1)} %refs_0_.1), channel_id=1, source_target_pairs={{0,1},{1,2},{2,3},{3,0},{4,5},{5,6},{6,7},{7,4},{8,9},{9,10},{10,1... | collective-permute-start | bytes 7077896 | tf_op jit(solution)/shard_map/ppermute | solution.py:255
  10.2 127.7 %collective-permute-start.1 = (bf16[384,3072]{1,0:T(8,128)(2,1)}, bf16[384,3072]{1,0:T(8,128)(2,1)}, u32[]{:S(2)}, u32[]{:S(2)}) collective-permute-start(bf16[384,3072]{1,0:T(8,128)(2,1)} %refs_0_.1), channel_id=1, source_target_pairs={{0,2},{1,3},{2,0},{3,1},{4,6},{5,7},{6,4},{7,5},{8,10},{9,11},{10,... | collective-permute-start | bytes 7077896 | tf_op jit(solution)/shard_map/ppermute | solution.py:255
  13.0 125.0 %collective-permute-start.2 = (bf16[384,3072]{1,0:T(8,128)(2,1)}, bf16[384,3072]{1,0:T(8,128)(2,1)}, u32[]{:S(2)}, u32[]{:S(2)}) collective-permute-start(bf16[384,3072]{1,0:T(8,128)(2,1)} %refs_0_.1), channel_id=1, source_target_pairs={{0,3},{1,0},{2,1},{3,2},{4,7},{5,4},{6,5},{7,6},{8,11},{9,8},{10,9... | collective-permute-start | bytes 7077896 | tf_op jit(solution)/shard_map/ppermute | solution.py:255
  15.6 50.9 %collective-permute-start.3 = (bf16[32,3072]{1,0:T(8,128)(2,1)}, bf16[32,3072]{1,0:T(8,128)(2,1)}, u32[]{:S(2)}, u32[]{:S(2)}) collective-permute-start(bf16[32,3072]{1,0:T(8,128)(2,1)} %dynamic-slice_bitcast_fusion), channel_id=1, source_target_pairs={{0,4},{4,0},{1,5},{5,1},{2,6},{6,2},{3,7},{7,3},{8,12},{12,8},{9,1... | collective-permute-start | bytes 589832 | tf_op jit(solution)/shard_map/ppermute | solution.py:263
  35.5 29.5 %collective-permute-start.4 = (f32[3,3072]{1,0:T(4,128)}, f32[3,3072]{1,0:T(4,128)}, u32[]{:S(2)}, u32[]{:S(2)}) collective-permute-start(f32[3,3072]{1,0:T(4,128)} %pad_maximum_fusion.4), channel_id=1, source_target_pairs={{0,4},{4,0},{1,5},{5,1},{2,6},{6,2},{3,7},{7,3},{8,12},{12,8},{9,1... | collective-permute-start | bytes 110600 | tf_op jit(solution)/shard_map/ppermute | solution.py:265
  35.5 10.4 %copy-start.11 = (bf16[1,256,3072]{2,1,0:T(8,128)(2,1)S(1)}, bf16[1,256,3072]{2,1,0:T(8,128)(2,1)}, u32[]{:S(2)}) copy-start(bf16[1,256,3072]{2,1,0:T(8,128)(2,1)} %param.17) | copy-start | bytes 4718596
  46.8 5.5 %copy-start.12 = (bf16[1,16,3072]{2,1,0:T(8,128)(2,1)S(1)}, bf16[1,16,3072]{2,1,0:T(8,128)(2,1)}, u32[]{:S(2)}) copy-start(bf16[1,16,3072]{2,1,0:T(8,128)(2,1)} %param.18) | copy-start | bytes 294916
  52.7 5.1 %copy-start.17 = (f32[128]{0:T(128)S(1)}, f32[128]{0:T(128)}, u32[]{:S(2)}) copy-start(f32[128]{0:T(128)} %param.21) | copy-start | bytes 1540
  52.7 5.2 %copy-start.16 = (f32[128]{0:T(128)S(1)}, f32[128]{0:T(128)}, u32[]{:S(2)}) copy-start(f32[128]{0:T(128)} %param.22) | copy-start | bytes 1540
  57.7 1.0 copy-start.14
  58.4 5.4 %copy-start.13 = (bf16[3072,64]{0,1:T(8,128)(2,1)S(1)}, bf16[3072,64]{0,1:T(8,128)(2,1)}, u32[]{:S(2)}) copy-start(bf16[3072,64]{0,1:T(8,128)(2,1)} %param.27) | copy-start | bytes 1179652
  58.6 6.4 %copy-start.15 = (f32[1,2,3072]{2,1,0:T(2,128)S(1)}, f32[1,2,3072]{2,1,0:T(2,128)}, u32[]{:S(2)}) copy-start(f32[1,2,3072]{2,1,0:T(2,128)} %param.26) | copy-start | bytes 73732
  110.6 2.9 %copy-start = (bf16[16,544,384]{2,1,0:T(8,128)(2,1)S(1)}, bf16[16,544,384]{2,1,0:T(8,128)(2,1)}, u32[]{:S(2)}) copy-start(bf16[16,544,384]{2,1,0:T(8,128)(2,1)} %all-gather.2.cloned.1.call-done) | copy-start | bytes 20054020
  113.5 1.0 copy-start.2
  114.5 28.3 %copy-start.1 = (bf16[384,3072]{1,0:T(8,128)(2,1)S(1)}, bf16[384,3072]{1,0:T(8,128)(2,1)}, u32[]{:S(2)}) copy-start(bf16[384,3072]{1,0:T(8,128)(2,1)} %refs_0_.1) | copy-start | bytes 7077892
  114.5 28.3 %copy-start.6 = (f32[32,64]{1,0:T(8,128)S(1)}, f32[32,64]{1,0:T(8,128)}, u32[]{:S(2)}) copy-start(f32[32,64]{1,0:T(8,128)} %refs_11_.1) | copy-start | bytes 24580
  131.1 11.7 %all-to-all-start = ((bf16[8,32,384]{2,1,0:T(8,128)(2,1)}), bf16[8,32,384]{2,1,0:T(8,128)(2,1)}, u32[]{:S(2)}, u32[]{:S(2)}) async-start(bf16[8,32,384]{2,1,0:T(8,128)(2,1)} %bitcast.33), calls=%async_computation | async-start | bytes 393216 | tf_op jit(solution)/shard_map/all_to_all | solution.py:307
  142.8 0.7 copy-start.3
  143.5 0.7 copy-start.4
  144.3 0.7 copy-start.5
  145.0 0.7 copy-start.7
  145.7 0.7 copy-start.8
  146.4 0.7 copy-start.9
  147.1 0.7 copy-start.10
Sparse Core Ops, SparseCore 0:
  9.8 100.7 all-gather.1
